TPU v7x, 32 devices: a whole 2x2x4 slice. The times are simulated.
32 devices in a mesh: group: 4 (over x, core), tensor: 8 (over z, y).
Axes of the slice: x: 2, y: 2, z: 4, core: 2. Of those that a mesh axis runs over, the one named last changes fastest.
Arguments:
- tokens: bfloat16 [128, 3, 8192], P(('group', 'tensor')), may hold values from -6 to 6
- norm_gain: float32 [8192], replicated, may hold values from 0.25 to 1.75
- w_qkv: bfloat16 [8192, 10240], P(None, 'tensor'), may hold values from -0.0625 to 0.0625
- w_out: bfloat16 [8192, 8192], P('tensor'), may hold values from -0.0625 to 0.0625
- lengths: int32 [32, 4], P(('group', 'tensor')), may hold values from 1 to 512, 1024 in all within a row
- migrate: int32 [32, 4], P(('group', 'tensor')), may hold values from 0 to 3, as said below
- page_order: int32 [32, 12], P(('group', 'tensor')), may hold values from 0 to 11, each once within a row
- kv_pool: bfloat16 [32, 12, 2, 8, 128, 128], P(('group', 'tensor')), as said below
Outputs:
- mixed: bfloat16 [128, 3, 8192], P(('group', 'tensor'))
Inputs may be any that keep to these rules, and one draw needn't show every extreme that they name: `migrate`: on each device every group number is named by exactly 1 row. The 4 lengths of one device sum to 1024. `kv_pool`: cached keys and values of order one or more.
All inputs are finite; a program needn't handle non-finite values.
Results may differ from a plain program's by a relative error of at most 0.013.
Values may be sent and summed in bfloat16 or wider, within the bound.
No kernel may reach another device: no remote copies, remote signals or barrier semaphores. Data moves between devices by JAX's collectives and lax.ppermute only.
A program may use at most 128 MiB of HBM per device.

v0:
```python
import jax
import jax.numpy as jnp
from jax import lax
from jax.sharding import PartitionSpec as P

HEADS = 64
KV_HEADS = 8
HEAD_DIM = 128
PAGE = 128
MAX_PAGES = 4
EPS = 1e-05
ROPE_BASE = 500000.0
NEG_FILL = -1e30


def rotate(values, positions):
    half_dim = values.shape[-1] // 2
    inverse = ROPE_BASE ** (-(jnp.arange(half_dim, dtype=jnp.float32) * 2.0 / values.shape[-1]))
    angles = positions.astype(jnp.float32)[..., None] * inverse
    cosine = jnp.cos(angles)[..., None, :]
    sine = jnp.sin(angles)[..., None, :]
    lower_half = values[..., :half_dim]
    upper_half = values[..., half_dim:]
    return jnp.concatenate(
        [lower_half * cosine - upper_half * sine, upper_half * cosine + lower_half * sine], axis=-1
    )


def cache_stats(queries, pages, row_lens):
    row_total, steps_here, head_count, head_dim = queries.shape
    page_count = pages.shape[1]
    kv_heads = pages.shape[3]
    page_len = pages.shape[4]
    grouped = queries.reshape(row_total, steps_here, kv_heads, head_count // kv_heads, head_dim)
    scores = jnp.einsum(
        "rskgd,rbktd->rskgbt", grouped, pages[:, :, 0], preferred_element_type=jnp.float32
    ) * head_dim ** (-0.5)
    places = (
        jnp.arange(page_count, dtype=jnp.int32)[:, None] * page_len
        + jnp.arange(page_len, dtype=jnp.int32)[None, :]
    )
    inside = (places[None] < row_lens[:, None, None])[:, None, None, None]
    page_top = jnp.max(jnp.where(inside, scores, NEG_FILL), axis=-1)
    weights = jnp.where(inside, jnp.exp(scores - page_top[..., None]), 0.0).astype(jnp.bfloat16)
    page_total = jnp.sum(weights.astype(jnp.float32), axis=-1)
    page_acc = jnp.einsum(
        "rskgbt,rbktd->rskgbd", weights, pages[:, :, 1], preferred_element_type=jnp.float32
    )
    top_score = jnp.max(page_top, axis=-1)
    page_scale = jnp.exp(page_top - top_score[..., None])
    return (
        top_score,
        jnp.sum(page_scale * page_total, axis=-1),
        jnp.sum(page_scale[..., None] * page_acc, axis=-2),
    )


def finish(queries, cache_parts, all_keys, all_values):
    row_total, steps_here, head_count, head_dim = queries.shape
    kv_heads = all_keys.shape[2]
    grouped = queries.reshape(row_total, steps_here, kv_heads, head_count // kv_heads, head_dim)
    scores = jnp.einsum(
        "rskgd,rukd->rskgu", grouped, all_keys, preferred_element_type=jnp.float32
    ) * head_dim ** (-0.5)
    allowed = jnp.arange(all_keys.shape[1])[None, :] <= jnp.arange(steps_here)[:, None]
    allowed = allowed[None, :, None, None, :]
    new_top = jnp.max(jnp.where(allowed, scores, NEG_FILL), axis=-1)
    weights = jnp.where(allowed, jnp.exp(scores - new_top[..., None]), 0.0).astype(jnp.bfloat16)
    new_total = jnp.sum(weights.astype(jnp.float32), axis=-1)
    new_acc = jnp.einsum(
        "rskgu,rukd->rskgd", weights, all_values, preferred_element_type=jnp.float32
    )
    cache_top, cache_total, cache_acc = cache_parts
    top_score = jnp.maximum(cache_top, new_top)
    cache_scale = jnp.exp(cache_top - top_score)
    new_scale = jnp.exp(new_top - top_score)
    merged = (cache_scale[..., None] * cache_acc + new_scale[..., None] * new_acc) / (
        cache_scale * cache_total + new_scale * new_total
    )[..., None]
    return merged.reshape(row_total, steps_here, head_count * head_dim).astype(jnp.bfloat16)


def per_device(tokens, norm_gain, w_qkv, w_out, lengths, migrate, page_order, kv_pool):
    row_lens = lengths[0]
    destinations = migrate[0]
    pool_order = page_order[0]
    page_pool = kv_pool[0]
    row_total = row_lens.shape[0]
    pool_size = page_pool.shape[0]
    slot_ids = jnp.arange(row_total, dtype=jnp.int32)
    sort_keys = destinations * row_total + slot_ids
    row_ranks = jnp.sum((sort_keys[None, :] < sort_keys[:, None]).astype(jnp.int32), axis=1)
    placing = row_ranks[:, None] == slot_ids[None, :]
    pages_used = (row_lens + PAGE - 1) // PAGE
    offsets = jnp.cumsum(pages_used) - pages_used
    sorted_lens = jnp.sum(jnp.where(placing, row_lens[:, None], 0), axis=0)
    sorted_first = jnp.sum(jnp.where(placing, offsets[:, None], 0), axis=0)
    page_slots = jnp.clip(
        sorted_first[:, None] + jnp.arange(MAX_PAGES, dtype=jnp.int32)[None, :], 0, pool_size - 1
    )
    home_pages = page_pool[pool_order[page_slots]]
    new_lens = lax.all_to_all(sorted_lens, "group", split_axis=0, concat_axis=0, tiled=True)
    moved_pages = lax.all_to_all(home_pages, "group", split_axis=0, concat_axis=0, tiled=True)
    width_q = HEADS * HEAD_DIM
    width_k = KV_HEADS * HEAD_DIM
    keys_so_far = jnp.zeros((row_total, 0, KV_HEADS, HEAD_DIM), jnp.bfloat16)
    values_so_far = jnp.zeros((row_total, 0, KV_HEADS, HEAD_DIM), jnp.bfloat16)
    steps_here = tokens.shape[1]
    floats = tokens.astype(jnp.float32)
    normed = (
        floats * lax.rsqrt(jnp.mean(floats * floats, axis=-1, keepdims=True) + EPS) * norm_gain
    ).astype(jnp.bfloat16)
    gathered = jnp.einsum(
        "rsd,dc->rsc",
        lax.all_gather(normed, "tensor", axis=0, tiled=True),
        w_qkv,
        preferred_element_type=jnp.float32,
    ).astype(jnp.bfloat16)
    full_rows = lax.all_to_all(gathered, "tensor", split_axis=0, concat_axis=2, tiled=True)
    positions = new_lens[:, None] + 0 + jnp.arange(steps_here, dtype=jnp.int32)[None, :]
    queries = rotate(
        full_rows[..., :width_q]
        .reshape(row_total, steps_here, HEADS, HEAD_DIM)
        .astype(jnp.float32),
        positions,
    ).astype(jnp.bfloat16)
    keys_here = rotate(
        full_rows[..., width_q : width_q + width_k]
        .reshape(row_total, steps_here, KV_HEADS, HEAD_DIM)
        .astype(jnp.float32),
        positions,
    ).astype(jnp.bfloat16)
    values_here = full_rows[..., width_q + width_k :].reshape(
        row_total, steps_here, KV_HEADS, HEAD_DIM
    )
    all_keys = jnp.concatenate([keys_so_far, keys_here], axis=1)
    all_values = jnp.concatenate([values_so_far, values_here], axis=1)
    attended = finish(queries, cache_stats(queries, moved_pages, new_lens), all_keys, all_values)
    spread = lax.all_to_all(attended, "tensor", split_axis=2, concat_axis=0, tiled=True)
    summed = lax.psum_scatter(
        jnp.einsum("rsc,cd->rsd", spread, w_out, preferred_element_type=jnp.float32).astype(
            jnp.bfloat16
        ),
        "tensor",
        scatter_dimension=0,
        tiled=True,
    ).astype(jnp.float32)
    output = (floats + summed).astype(jnp.bfloat16)
    return output


def solution(mesh):
    in_specs = (
        P(("group", "tensor"), None, None),
        P(),
        P(None, "tensor"),
        P("tensor", None),
        P(("group", "tensor"), None),
        P(("group", "tensor"), None),
        P(("group", "tensor"), None),
        P(("group", "tensor"), None, None, None, None, None),
    )
    out_specs = P(("group", "tensor"), None, None)
    return jax.shard_map(
        per_device, mesh=mesh, in_specs=in_specs, out_specs=out_specs, check_vma=False
    )
```

profile of v0, /device:TPU:0, one launch (start us, length us, event | category | flops | bytes accessed | tf_op | source)
XLA Modules:
  0.0 357.1 jit_solution(14385449491544345333)
XLA Ops:
  6.5 1.1 fusion.25
  7.7 1.1 fusion.27
  8.8 0.9 copy.104
  9.7 0.7 and_select_fusion.1
  10.6 0.7 add_bitcast_fusion
  11.2 0.7 bitcast_add_fusion
  12.1 0.7 bitcast_subtract_fusion.1
  12.7 0.7 select_reduce_fusion.2
  13.5 0.7 copy.101
  14.1 4.2 %all-to-all-start = ((s32[4,1,1]{2,1,0:T(1,128)}), s32[4,1,1]{2,1,0:T(1,128)S(1)}, u32[]{:S(2)}, u32[]{:S(2)}) async-start(s32[4,1,1]{2,1,0:T(1,128)} %copy.101), calls=%async_computation | async-start | bytes 4096 | tf_op jit(solution)/shard_map/all_to_all | solution.py:102
  18.5 43.2 %all-gather.2.cloned.1.call-done = bf16[32,3,8192]{2,1,0:T(4,128)(2,1)} async-done(((bf16[4,3,8192]{2,1,0:T(4,128)(2,1)}), bf16[32,3,8192]{2,1,0:T(4,128)(2,1)}) %all-gather.2.cloned.1.call-update) | async-done | bytes 1572880 | tf_op jit(solution)/shard_map/all_gather | solution.py:115
  61.7 12.2 %fusion.9 = bf16[32,3,1280]{2,0,1:T(8,128)(2,1)S(1)} fusion(bf16[8192,1280]{1,0:T(8,128)(2,1)} %param.10, bf16[32,3,8192]{2,1,0:T(4,128)(2,1)} %all-gather.2.cloned.1.call-done), kind=kOutput, calls=%fused_computation.11 | convolution fusion | flops 2013388800 | bytes 22790144 | tf_op jit(solution)/shard_map/rsd,dc->rsc/dot_general | solution.py:113
  73.9 0.9 copy.106
  74.8 3.4 all-to-all-start.2
  78.3 0.7 gather_fusion
  79.2 7.5 %gather_fusion.1 = bf16[16,2,8,128,128]{4,3,2,1,0:T(8,128)(2,1)} fusion(bf16[12,2,8,128,128]{4,3,2,1,0:T(8,128)(2,1)} %bitcast.134, s32[1024]{0:T(1024)S(1)} %pad_clamp_fusion), kind=kCustom, calls=%fused_computation.1 | custom fusion | bytes 16777280 | tf_op jit(solution)/shard_map/gather | solution.py:101
  86.7 10.3 %copy.102 = bf16[4,4,2,8,128,128]{5,4,1,3,2,0:T(8,128)(2,1)} copy(bf16[4,4,2,8,128,128]{5,4,3,2,1,0:T(8,128)(2,1)} %bitcast.131) | data formatting | bytes 16777216 | tf_op jit(solution)/shard_map/gather | solution.py:101
  97.0 5.7 %all-to-all-start.1 = ((bf16[4,4,2,8,128,128]{5,4,1,3,2,0:T(8,128)(2,1)}), bf16[4,4,2,8,128,128]{5,4,1,3,2,0:T(8,128)(2,1)}, u32[]{:S(2)}, u32[]{:S(2)}) async-start(bf16[4,4,2,8,128,128]{5,4,1,3,2,0:T(8,128)(2,1)} %copy.102), calls=%async_computation.1 | async-start | bytes 16777216 | tf_op jit(solution)/shard_map/all_to_all | solution.py:103
  104.6 0.8 select_reduce_fusion
  105.7 90.2 %all-to-all-done.1 = bf16[4,4,2,8,128,128]{5,4,1,3,2,0:T(8,128)(2,1)} async-done(((bf16[4,4,2,8,128,128]{5,4,1,3,2,0:T(8,128)(2,1)}), bf16[4,4,2,8,128,128]{5,4,1,3,2,0:T(8,128)(2,1)}, u32[]{:S(2)}, u32[]{:S(2)}) %all-to-all-start.1) | async-done | bytes 8388640 | tf_op jit(solution)/shard_map/all_to_all | solution.py:103
  195.9 3.6 %fusion.17 = (f32[4,3,8,8,4]{3,1,4,2,0:T(4,128)S(1)}, f32[4,8,4,128,3,8]{3,5,4,2,1,0:T(8,128)S(1)}) fusion(pred[4,4,128]{2,1,0:T(4,128)(4,1)S(1)} %broadcast_compare_fusion, bf16[4,4,2,8,128,128]{5,4,1,3,2,0:T(8,128)(2,1)} %all-to-all-done.1, bf16[4,3,8,8,64]{4,3,2,0,1:T(8,128)(2,1)S(1)} %get-tuple-element.15, ...), kind=kOutput, calls=%fused_computation.21 | convolution fusion | flops 102233088 | bytes 5978112 | tf_op jit(solution)/shard_map/rskgd,rbktd->rskgbt/dot_general | solution.py:35
  199.5 1.2 convert_reduce_fusion
  201.0 3.6 fusion.12
  205.2 6.5 %copy.134 = bf16[4,3,8,8,128]{0,1,4,3,2:T(4,128)(2,1)} copy(bf16[4,3,8,8,128]{4,3,1,2,0:T(8,128)(2,1)S(1)} %fusion.23) | data formatting | bytes 393216 | tf_op jit(solution)/shard_map/convert_element_type | solution.py:80
  211.7 9.7 %reshape.316 = bf16[8,2,6144]{2,1,0:T(2,128)(2,1)S(1)} reshape(bf16[8192,3,4]{2,1,0:T(4,128)(2,1)} %bitcast.132) | data formatting | bytes 393216
  221.4 13.5 %all_to_all.50 = bf16[8,2,6144]{2,1,0:T(2,128)(2,1)S(1)} all-to-all(bf16[8,2,6144]{2,1,0:T(2,128)(2,1)S(1)} %reshape.316), channel_id=1, replica_groups=mesh['group'=4,'tensor'=8] {'tensor'}, dimensions={0} | all-to-all | bytes 393216 | tf_op jit(solution)/shard_map/all_to_all | solution.py:139
  234.9 8.5 %reshape.317 = bf16[8192,3,4]{2,1,0:T(4,128)(2,1)} reshape(bf16[8,2,6144]{2,1,0:T(2,128)(2,1)S(1)} %all_to_all.50) | data formatting | bytes 393216
  243.4 7.9 %copy.135 = bf16[4,3,8,1024]{3,2,0,1:T(8,128)(2,1)S(1)} copy(bf16[4,3,8,1024]{0,1,3,2:T(4,128)(2,1)} %bitcast.133) | data formatting | bytes 393216 | tf_op jit(solution)/shard_map/all_to_all | solution.py:139
  251.6 9.7 %fusion.4 = bf16[32,3,8192]{2,0,1:T(8,128)(2,1)} fusion(bf16[32,3,1024]{2,0,1:T(8,128)(2,1)S(1)} %all_to_all.45, bf16[1024,8192]{1,0:T(8,128)(2,1)} %param.11), kind=kOutput, calls=%fused_computation.6 | convolution fusion | flops 1611399168 | bytes 18546688 | tf_op jit(solution)/shard_map/rsc,cd->rsd/dot_general | solution.py:141
  261.3 0.6 copy-done.3
  263.2 85.3 %all-reduce.3.cloned.1.call-done = bf16[32,3,8192]{2,0,1:T(8,128)(2,1)} async-done(((bf16[32,3,8192]{2,0,1:T(8,128)(2,1)}), bf16[32,3,8192]{2,0,1:T(8,128)(2,1)}) %all-reduce.3.cloned.1.call-update) | async-done | bytes 1572880
  348.4 1.8 fusion.28
  (50 shorter events, 4.4 us)
Async XLA Ops:
  6.5 71.8 %copy-start = (s32[1,12]{1,0:T(1,128)S(1)}, s32[1,12]{1,0:T(1,128)}, u32[]{:S(2)}) copy-start(s32[1,12]{1,0:T(1,128)} %param.14) | copy-start | bytes 148
  6.5 55.2 %all-gather.2.cloned.1.call-start = ((), (), s32[]{:S(2)}) async-start(), calls=%async_computation.4 | async-start | bytes 2359296 | tf_op jit(solution)/shard_map/all_gather | solution.py:115
  14.1 60.7 %all-to-all-start = ((s32[4,1,1]{2,1,0:T(1,128)}), s32[4,1,1]{2,1,0:T(1,128)S(1)}, u32[]{:S(2)}, u32[]{:S(2)}) async-start(s32[4,1,1]{2,1,0:T(1,128)} %copy.101), calls=%async_computation | async-start | bytes 4096 | tf_op jit(solution)/shard_map/all_to_all | solution.py:102
  74.8 22.2 %all-to-all-start.2 = ((bf16[32,3,1280]{2,1,0:T(4,128)(2,1)}), bf16[32,3,1280]{2,1,0:T(4,128)(2,1)S(1)}, u32[]{:S(2)}, u32[]{:S(2)}) async-start(bf16[32,3,1280]{2,1,0:T(4,128)(2,1)} %copy.106), calls=%async_computation.2 | async-start | bytes 655360 | tf_op jit(solution)/shard_map/all_to_all | solution.py:119
  97.0 98.8 %all-to-all-start.1 = ((bf16[4,4,2,8,128,128]{5,4,1,3,2,0:T(8,128)(2,1)}), bf16[4,4,2,8,128,128]{5,4,1,3,2,0:T(8,128)(2,1)}, u32[]{:S(2)}, u32[]{:S(2)}) async-start(bf16[4,4,2,8,128,128]{5,4,1,3,2,0:T(8,128)(2,1)} %copy.102), calls=%async_computation.1 | async-start | bytes 16777216 | tf_op jit(solution)/shard_map/all_to_all | solution.py:103
  102.8 245.7 %all-reduce.3.cloned.1.call-start = ((), (), s32[]{:S(2)}) async-start(), calls=%async_computation.5 | async-start | bytes 3145728
  251.5 98.7 %copy-start.1 = (s32[1,12]{1,0:T(1,128)S(1)}, s32[1,12]{1,0:T(1,128)}, u32[]{:S(2)}) copy-start(s32[1,12]{1,0:T(1,128)} %param.14) | copy-start | bytes 148
  261.3 0.7 copy-start.3
  261.3 87.2 %copy-start.2 = (bf16[4,3,8192]{2,0,1:T(4,128)(2,1)S(1)}, bf16[4,3,8192]{2,0,1:T(4,128)(2,1)}, u32[]{:S(2)}) copy-start(bf16[4,3,8192]{2,0,1:T(4,128)(2,1)} %param.8) | copy-start | bytes 589828
Sparse Core Ops, SparseCore 0:
  9.8 51.8 all-gather.1
  261.4 86.9 all-reduce.2
where the time goes:
time: 358 us; the launch traced here: 357 us
  waiting for transfers between devices  219 us (61%)
  local copies, waits for them, and re-layouts  56 us (16%)
  matrix products  30.5 us (9%)
  between operations  14.3 us (4%)
  starting transfers between devices  13.6 us (4%)
  blocking collectives  13.5 us (4%)
  other arithmetic  10.5 us (3%)
    all_to_all x1, waiting for transfers between devices, per_device(): lax.all_to_all(home_pages, 'group', split_axis=0, concat_axis=0, tiled=True)  90.2 us
    unnamed x3, waiting for transfers between devices  85.3 us
    all_gather x1, waiting for transfers between devices, per_device(): lax.all_gather(normed, 'tensor', axis=0, tiled=True)  43.2 us
    unnamed x11, local copies, waits for them, and re-layouts  19.4 us
    gather x4, local copies, waits for them, and re-layouts, per_device(): home_pages = page_pool[pool_order[page_slots]]  18.6 us
    all_to_all x1, blocking collectives, per_device(): lax.all_to_all(attended, 'tensor', split_axis=2, concat_axis=0, tiled=True)  13.5 us
    dot_general x1, matrix products, per_device(): jnp.einsum('rsd,dc->rsc', lax.all_gather(normed, 'tensor', axis=0, tiled=...  12.2 us
    dot_general x1, matrix products, per_device(): jnp.einsum('rsc,cd->rsd', spread, w_out, preferred_element_type=jnp.float32)  9.71 us
  transfers between devices with their start and end apart: 5, of which 3 were waited for; matrix products, arithmetic and copies ran while one was open for 11% of the time, Pallas kernels for 0%

commit v1 on v0

--- a/solution.py
+++ b/solution.py
@@ -11,6 +11,13 @@
 EPS = 1e-05
 ROPE_BASE = 500000.0
 NEG_FILL = -1e30
+
+
+def swap_blocks(block, mesh_axis, split, join):
+    n_dev = lax.axis_size(mesh_axis)
+    blocks = jnp.stack(jnp.split(block, n_dev, axis=split), axis=0)
+    blocks = lax.all_to_all(blocks, mesh_axis, split_axis=0, concat_axis=0)
+    return jnp.concatenate(blocks, axis=join)
 
 
 def rotate(values, positions):
@@ -136,7 +143,7 @@
     all_keys = jnp.concatenate([keys_so_far, keys_here], axis=1)
     all_values = jnp.concatenate([values_so_far, values_here], axis=1)
     attended = finish(queries, cache_stats(queries, moved_pages, new_lens), all_keys, all_values)
-    spread = lax.all_to_all(attended, "tensor", split_axis=2, concat_axis=0, tiled=True)
+    spread = swap_blocks(attended, "tensor", 2, 0)
     summed = lax.psum_scatter(
         jnp.einsum("rsc,cd->rsd", spread, w_out, preferred_element_type=jnp.float32).astype(
             jnp.bfloat16

time: 358 us -> 325 us (0.908)
  local copies, waits for them, and re-layouts: 56 us -> 23.5 us
    unnamed x11 -> x16, local copies, waits for them, and re-layouts: 19.4 us -> 1.35 us
    all_to_all x3 -> x1, local copies, waits for them, and re-layouts: 8.09 us -> 0.07 us  [swap_blocks(): blocks = lax.all_to_all(blocks, mesh_axis, split_axis=0, concat_axis=0)]
    convert_element_type x1 -> x2, local copies, waits for them, and re-layouts: 6.53 us -> 0.09 us  [finish(): merged.reshape(row_total, steps_here, head_count * head_dim)]
  transfers between devices with their start and end apart: 5 -> 5, of which waited for: 3 -> 3; matrix products, arithmetic and copies ran while one was open for 11% -> 12% of each run, Pallas kernels for 0% -> 0%
where the time goes in v1:
time: 325 us
  waiting for transfers between devices  219 us (67%)
  matrix products  30.5 us (9%)
  local copies, waits for them, and re-layouts  23.5 us (7%)
  between operations  14.3 us (4%)
  starting transfers between devices  13.6 us (4%)
  blocking collectives  13.5 us (4%)
  other arithmetic  10.5 us (3%)
    all_to_all x1, waiting for transfers between devices, per_device(): lax.all_to_all(home_pages, 'group', split_axis=0, concat_axis=0, tiled=True)  90.2 us
    unnamed x3, waiting for transfers between devices  85.3 us
    all_gather x1, waiting for transfers between devices, per_device(): lax.all_gather(normed, 'tensor', axis=0, tiled=True)  43.2 us
    gather x4, local copies, waits for them, and re-layouts, per_device(): home_pages = page_pool[pool_order[page_slots]]  18.6 us
    all_to_all x1, blocking collectives, swap_blocks(): blocks = lax.all_to_all(blocks, mesh_axis, split_axis=0, concat_axis=0)  13.5 us
    dot_general x1, matrix products, per_device(): jnp.einsum('rsd,dc->rsc', lax.all_gather(normed, 'tensor', axis=0, tiled=...  12.2 us
    dot_general x1, matrix products, per_device(): jnp.einsum('rsc,cd->rsd', spread, w_out, preferred_element_type=jnp.float32)  9.71 us
  transfers between devices with their start and end apart: 5, of which 3 were waited for; matrix products, arithmetic and copies ran while one was open for 12% of the time, Pallas kernels for 0%

profile of v1, /device:TPU:0, one launch (start us, length us, event | category | flops | bytes accessed | tf_op | source)
XLA Modules:
  0.0 324.6 jit_solution(14657102957977391440)
XLA Ops:
  6.5 1.1 fusion.25
  7.7 1.1 fusion.27
  8.8 0.9 copy.105
  9.7 0.7 and_select_fusion.1
  10.6 0.7 add_bitcast_fusion
  11.2 0.7 bitcast_add_fusion
  12.1 0.7 bitcast_subtract_fusion.1
  12.7 0.7 select_reduce_fusion.2
  13.5 0.7 copy.102
  14.1 4.2 %all-to-all-start = ((s32[4,1,1]{2,1,0:T(1,128)}), s32[4,1,1]{2,1,0:T(1,128)S(1)}, u32[]{:S(2)}, u32[]{:S(2)}) async-start(s32[4,1,1]{2,1,0:T(1,128)} %copy.102), calls=%async_computation | async-start | bytes 4096 | tf_op jit(solution)/shard_map/all_to_all | solution.py:109
  18.5 43.2 %all-gather.2.cloned.1.call-done = bf16[32,3,8192]{2,1,0:T(4,128)(2,1)} async-done(((bf16[4,3,8192]{2,1,0:T(4,128)(2,1)}), bf16[32,3,8192]{2,1,0:T(4,128)(2,1)}) %all-gather.2.cloned.1.call-update) | async-done | bytes 1572880 | tf_op jit(solution)/shard_map/all_gather | solution.py:122
  61.7 12.2 %fusion.9 = bf16[32,3,1280]{2,0,1:T(8,128)(2,1)S(1)} fusion(bf16[8192,1280]{1,0:T(8,128)(2,1)} %param.10, bf16[32,3,8192]{2,1,0:T(4,128)(2,1)} %all-gather.2.cloned.1.call-done), kind=kOutput, calls=%fused_computation.11 | convolution fusion | flops 2013388800 | bytes 22790144 | tf_op jit(solution)/shard_map/rsd,dc->rsc/dot_general | solution.py:120
  73.9 0.9 copy.107
  74.8 3.4 %all-to-all-start.2 = ((bf16[32,3,1280]{2,1,0:T(4,128)(2,1)}), bf16[32,3,1280]{2,1,0:T(4,128)(2,1)S(1)}, u32[]{:S(2)}, u32[]{:S(2)}) async-start(bf16[32,3,1280]{2,1,0:T(4,128)(2,1)} %copy.107), calls=%async_computation.2 | async-start | bytes 655360 | tf_op jit(solution)/shard_map/all_to_all | solution.py:126
  78.3 0.7 gather_fusion
  79.2 7.5 %gather_fusion.1 = bf16[16,2,8,128,128]{4,3,2,1,0:T(8,128)(2,1)} fusion(bf16[12,2,8,128,128]{4,3,2,1,0:T(8,128)(2,1)} %bitcast.163, s32[1024]{0:T(1024)S(1)} %pad_clamp_fusion), kind=kCustom, calls=%fused_computation.1 | custom fusion | bytes 16777280 | tf_op jit(solution)/shard_map/gather | solution.py:108
  86.7 10.3 %copy.103 = bf16[4,4,2,8,128,128]{5,4,1,3,2,0:T(8,128)(2,1)} copy(bf16[4,4,2,8,128,128]{5,4,3,2,1,0:T(8,128)(2,1)} %bitcast.162) | data formatting | bytes 16777216 | tf_op jit(solution)/shard_map/gather | solution.py:108
  97.0 5.7 %all-to-all-start.1 = ((bf16[4,4,2,8,128,128]{5,4,1,3,2,0:T(8,128)(2,1)}), bf16[4,4,2,8,128,128]{5,4,1,3,2,0:T(8,128)(2,1)}, u32[]{:S(2)}, u32[]{:S(2)}) async-start(bf16[4,4,2,8,128,128]{5,4,1,3,2,0:T(8,128)(2,1)} %copy.103), calls=%async_computation.1 | async-start | bytes 16777216 | tf_op jit(solution)/shard_map/all_to_all | solution.py:110
  103.9 0.3 reshape.288
  104.6 0.8 select_reduce_fusion
  105.4 0.2 convert_reduce_fusion.1
  105.7 90.2 %all-to-all-done.1 = bf16[4,4,2,8,128,128]{5,4,1,3,2,0:T(8,128)(2,1)} async-done(((bf16[4,4,2,8,128,128]{5,4,1,3,2,0:T(8,128)(2,1)}), bf16[4,4,2,8,128,128]{5,4,1,3,2,0:T(8,128)(2,1)}, u32[]{:S(2)}, u32[]{:S(2)}) %all-to-all-start.1) | async-done | bytes 8388640 | tf_op jit(solution)/shard_map/all_to_all | solution.py:110
  195.9 3.6 %fusion.17 = (f32[4,3,8,8,4]{3,1,4,2,0:T(4,128)S(1)}, f32[4,8,4,128,3,8]{3,5,4,2,1,0:T(8,128)S(1)}) fusion(pred[4,4,128]{2,1,0:T(4,128)(4,1)S(1)} %broadcast_compare_fusion, bf16[4,4,2,8,128,128]{5,4,1,3,2,0:T(8,128)(2,1)} %all-to-all-done.1, bf16[4,3,8,8,64]{4,3,2,0,1:T(8,128)(2,1)S(1)} %get-tuple-element.15, ...), kind=kOutput, calls=%fused_computation.21 | convolution fusion | flops 102233088 | bytes 5978112 | tf_op jit(solution)/shard_map/rskgd,rbktd->rskgbt/dot_general | solution.py:42
  199.5 1.2 convert_reduce_fusion
  201.0 3.6 %fusion.12 = f32[4,3,8,8,128]{4,3,1,2,0:T(8,128)S(1)} fusion(bf16[4,4,2,8,128,128]{5,4,1,3,2,0:T(8,128)(2,1)} %all-to-all-done.1, f32[4,3,8,8,4]{3,1,4,2,0:T(4,128)S(1)} %get-tuple-element.13, f32[4,8,4,128,3,8]{3,5,4,2,1,0:T(8,128)S(1)} %get-tuple-element.25, f32[4,3,8,8,4]{3,1,4,2,0:T(4,128)S(1)} %get-tuple-element.24, ...), kind=kOutput, calls=%fused_computation.13 | convolution fusion | flops 102531072 | bytes 6187008 | tf_op jit(solution)/shard_map/rskgbt,rbktd->rskgbd/dot_general | solution.py:53
  204.5 0.6 fusion.23
  205.4 13.5 %all_to_all.37 = bf16[8,4,3,1024]{3,1,2,0:T(4,128)(2,1)S(1)} all-to-all(bf16[8,4,3,1024]{3,1,2,0:T(4,128)(2,1)S(1)} %fusion.43), channel_id=1, replica_groups=mesh['group'=4,'tensor'=8] {'tensor'}, dimensions={0} | all-to-all | bytes 393216 | tf_op jit(solution)/shard_map/all_to_all | solution.py:19
  219.1 9.7 %fusion.4 = bf16[32,3,8192]{2,0,1:T(8,128)(2,1)} fusion(bf16[32,3,1024]{2,0,1:T(8,128)(2,1)S(1)} %reshape.287, bf16[1024,8192]{1,0:T(8,128)(2,1)} %param.11), kind=kOutput, calls=%fused_computation.6 | convolution fusion | flops 1611399168 | bytes 18546688 | tf_op jit(solution)/shard_map/rsc,cd->rsd/dot_general | solution.py:148
  228.8 0.6 copy-done.3
  229.5 0.6 dynamic-slice
  230.7 85.2 %all-reduce.3.cloned.1.call-done = bf16[32,3,8192]{2,0,1:T(8,128)(2,1)} async-done(((bf16[32,3,8192]{2,0,1:T(8,128)(2,1)}), bf16[32,3,8192]{2,0,1:T(8,128)(2,1)}) %all-reduce.3.cloned.1.call-update) | async-done | bytes 1572880
  316.0 1.8 fusion.28
  (56 shorter events, 2.8 us)
Async XLA Ops:
  6.5 71.8 %copy-start = (s32[1,12]{1,0:T(1,128)S(1)}, s32[1,12]{1,0:T(1,128)}, u32[]{:S(2)}) copy-start(s32[1,12]{1,0:T(1,128)} %param.14) | copy-start | bytes 148
  6.5 55.2 %all-gather.2.cloned.1.call-start = ((), (), s32[]{:S(2)}) async-start(), calls=%async_computation.4 | async-start | bytes 2359296 | tf_op jit(solution)/shard_map/all_gather | solution.py:122
  14.1 60.7 %all-to-all-start = ((s32[4,1,1]{2,1,0:T(1,128)}), s32[4,1,1]{2,1,0:T(1,128)S(1)}, u32[]{:S(2)}, u32[]{:S(2)}) async-start(s32[4,1,1]{2,1,0:T(1,128)} %copy.102), calls=%async_computation | async-start | bytes 4096 | tf_op jit(solution)/shard_map/all_to_all | solution.py:109
  74.8 22.2 %all-to-all-start.2 = ((bf16[32,3,1280]{2,1,0:T(4,128)(2,1)}), bf16[32,3,1280]{2,1,0:T(4,128)(2,1)S(1)}, u32[]{:S(2)}, u32[]{:S(2)}) async-start(bf16[32,3,1280]{2,1,0:T(4,128)(2,1)} %copy.107), calls=%async_computation.2 | async-start | bytes 655360 | tf_op jit(solution)/shard_map/all_to_all | solution.py:126
  97.0 98.8 %all-to-all-start.1 = ((bf16[4,4,2,8,128,128]{5,4,1,3,2,0:T(8,128)(2,1)}), bf16[4,4,2,8,128,128]{5,4,1,3,2,0:T(8,128)(2,1)}, u32[]{:S(2)}, u32[]{:S(2)}) async-start(bf16[4,4,2,8,128,128]{5,4,1,3,2,0:T(8,128)(2,1)} %copy.103), calls=%async_computation.1 | async-start | bytes 16777216 | tf_op jit(solution)/shard_map/all_to_all | solution.py:110
  102.8 213.2 %all-reduce.3.cloned.1.call-start = ((), (), s32[]{:S(2)}) async-start(), calls=%async_computation.5 | async-start | bytes 3145728
  219.1 98.7 %copy-start.1 = (s32[1,12]{1,0:T(1,128)S(1)}, s32[1,12]{1,0:T(1,128)}, u32[]{:S(2)}) copy-start(s32[1,12]{1,0:T(1,128)} %param.14) | copy-start | bytes 148
  228.8 0.7 copy-start.3
  228.8 87.1 %copy-start.2 = (bf16[4,3,8192]{2,0,1:T(4,128)(2,1)S(1)}, bf16[4,3,8192]{2,0,1:T(4,128)(2,1)}, u32[]{:S(2)}) copy-start(bf16[4,3,8192]{2,0,1:T(4,128)(2,1)} %param.8) | copy-start | bytes 589828
Sparse Core Ops, SparseCore 0:
  9.8 51.8 all-gather.1
  229.0 86.9 all-reduce.2
